TPU v7x, 32 devices: a whole 2x2x4 slice. The times are simulated.
32 devices in a mesh: rep: 2 (over y), seq: 4 (over z), head: 2 (over x), sub: 2 (over core).
Axes of the slice: x: 2, y: 2, z: 4, core: 2. Of those that a mesh axis runs over, the one named last changes fastest.
Arguments:
- tokens: bfloat16 [32, 4096], P(('rep', 'sub'), 'seq'), parts along dimension 0, may hold values from -260 to 260
- attn_gain: float32 [4096], P('seq'), may hold values from 0.1 to 1.9
- w_query: bfloat16 [4096, 4096], P('seq', 'head'), may hold values from -0.09375 to 0.09375
- key_projection_weight: bfloat16 [4096, 1024], P('seq', 'head'), may hold values from -0.375 to 0.375
- value_projection_weight: bfloat16 [4096, 1024], P('seq', 'head'), may hold values from -0.375 to 0.375
- w_attn_out: bfloat16 [4096, 4096], P('head', 'seq'), may hold values from -0.09375 to 0.09375
- cache_keys: bfloat16 [32, 8, 2048, 128], P(('rep', 'sub'), 'head', 'seq'), parts along dimension 0, may hold values from -2500 to 2500
- stored_value_cache: bfloat16 [32, 8, 2048, 128], P(('rep', 'sub'), 'head', 'seq'), parts along dimension 0, may hold values from -12 to 12
- lengths: int32 [32], P(('rep', 'sub')), parts along dimension 0, may hold values from 1024 to 2048
- positions: int32 [32], P(('rep', 'sub')), parts along dimension 0, may hold values from 0 to 2047
- mamba_gain: float32 [4096], replicated, may hold values from 0.1 to 1.9
- w_in: bfloat16 [2, 4096, 8192], P(None, None, ('seq', 'head')), may hold values from -0.09375 to 0.09375
- conv_weight: float32 [4, 8192], P(None, ('seq', 'head')), may hold values from -3 to 3
- conv_bias: float32 [8192], P(('seq', 'head')), may hold values from -0.5 to 0.5
- conv_state: float32 [32, 3, 8192], P(('rep', 'sub'), None, ('seq', 'head')), parts along dimension 0, may hold values from -6 to 6
- w_xproj: bfloat16 [8192, 288], P(('seq', 'head')), may hold values from -0.0625 to 0.0625
- w_dt: bfloat16 [256, 8192], P(None, ('seq', 'head')), may hold values from -0.375 to 0.375
- dt_bias: float32 [8192], P(('seq', 'head')), may hold values from -4 to 0
- a_log: float32 [16, 8192], P(None, ('seq', 'head')), may hold values from 0 to 2.77
- skip_gain: float32 [8192], P(('seq', 'head')), may hold values from 0.25 to 2
- ssm_state: float32 [32, 16, 8192], P(('rep', 'sub'), None, ('seq', 'head')), parts along dimension 0, may hold values from -6 to 6
- w_mamba_out: bfloat16 [8192, 4096], P(('seq', 'head')), may hold values from -0.09375 to 0.09375
Outputs:
- hidden_out: bfloat16 [32, 4096], P(('rep', 'sub'), 'seq'), parts along dimension 0
- new_state: float32 [32, 16, 8192], P(('rep', 'sub'), None, ('seq', 'head')), parts along dimension 0
There are 2 independent parts, one for each index of `rep`. A program takes and returns all parts, laid end to end along the dimension named above; an argument that names none is the same for every part. Nothing has to cross between parts.
Inputs may be any that keep to these rules, and one draw needn't show every extreme that they name: Cache positions p < lengths[b] hold sequence b's past keys and values; later positions are not attended.
All inputs are finite; a program needn't handle non-finite values.
Results may differ from a plain program's by a relative error of at most 0.015.
Values may be sent and summed in bfloat16 or wider, within the bound.
A program may use at most 128 MiB of HBM per device.

v0:
```python
import math

import jax
import jax.numpy as jnp
from jax import lax
from jax.sharding import PartitionSpec as P

norm_eps = 1e-05
masked_floor = -1e30
rope_base = 10000.0


def joined(value, axis, join):
    pieces = jax.tree.map(lambda part: lax.all_gather(part, axis), value)
    head = jax.tree.map(lambda part: part[0], pieces)
    tail = jax.tree.map(lambda part: part[1:], pieces)
    subtotal, _ = lax.scan(lambda subtotal, section: (join(subtotal, section), None), head, tail)
    return subtotal


def apply_rotary(vectors, positions):
    half_dim = vectors.shape[-1] // 2
    frequency = jnp.exp(
        -math.log(rope_base) * 2.0 * jnp.arange(half_dim, dtype=jnp.float32) / (2 * half_dim)
    )
    angles = positions.astype(jnp.float32)[:, None] * frequency[None, :]
    cosine = jnp.cos(angles)[:, None, :]
    sine_part = jnp.sin(angles)[:, None, :]
    first_half = vectors[..., :half_dim]
    second_half = vectors[..., half_dim:]
    return jnp.concatenate(
        [
            first_half * cosine - second_half * sine_part,
            second_half * cosine + first_half * sine_part,
        ],
        axis=-1,
    )


def join_partial(earlier, later):
    max_one, sum_one, acc_one = earlier
    max_two, sum_two, acc_two = later
    joined_max = jnp.maximum(max_one, max_two)
    factor_one = jnp.exp(max_one - joined_max)
    factor_two = jnp.exp(max_two - joined_max)
    return (
        joined_max,
        sum_one * factor_one + sum_two * factor_two,
        acc_one * factor_one[..., None] + acc_two * factor_two[..., None],
    )


def local(
    tokens,
    attn_gain,
    w_query,
    key_projection_weight,
    value_projection_weight,
    w_attn_out,
    cache_keys,
    stored_value_cache,
    lengths,
    positions,
    mamba_gain,
    w_in,
    conv_weight,
    conv_bias,
    conv_state,
    w_xproj,
    w_dt,
    dt_bias,
    a_log,
    skip_gain,
    ssm_state,
    w_mamba_out,
):
    batch_rows = tokens.shape[0]
    feature_cols = tokens.shape[1]
    head_dim = cache_keys.shape[3]
    kv_local = cache_keys.shape[1]
    ctx_local = cache_keys.shape[2]
    q_local = w_query.shape[1] // head_dim
    query_group_count = q_local // kv_local
    model_width = feature_cols * lax.axis_size("seq")
    token_float = tokens.astype(jnp.float32)
    lifted = (token_float * attn_gain[None, :]).astype(jnp.bfloat16)
    part_query = jnp.dot(lifted, w_query, preferred_element_type=jnp.float32)
    part_key = jnp.dot(lifted, key_projection_weight, preferred_element_type=jnp.float32)
    part_value = jnp.dot(lifted, value_projection_weight, preferred_element_type=jnp.float32)
    squares = jnp.sum(token_float * token_float, axis=1)
    sum_squares = lax.psum(squares, "seq")
    part_query, part_key, part_value = lax.psum((part_query, part_key, part_value), "seq")
    inv_rms = lax.rsqrt(sum_squares / model_width + norm_eps)
    query_vectors = apply_rotary(
        (part_query * inv_rms[:, None]).reshape(batch_rows, q_local, head_dim), positions
    ).astype(jnp.bfloat16)
    fresh_key_rows = apply_rotary(
        (part_key * inv_rms[:, None]).reshape(batch_rows, kv_local, head_dim), positions
    ).astype(jnp.bfloat16)
    fresh_value_rows = (
        (part_value * inv_rms[:, None]).reshape(batch_rows, kv_local, head_dim).astype(jnp.bfloat16)
    )
    grouped_queries = query_vectors.reshape(batch_rows, kv_local, query_group_count, head_dim)
    score_scale = head_dim ** (-0.5)
    scores = (
        jnp.einsum(
            "bhgd,bhtd->bhgt", grouped_queries, cache_keys, preferred_element_type=jnp.float32
        )
        * score_scale
    )
    slot_index = lax.axis_index("seq") * ctx_local + jnp.arange(ctx_local, dtype=jnp.int32)
    live_mask = slot_index[None, None, None, :] < lengths[:, None, None, None]
    local_max = jnp.max(jnp.where(live_mask, scores, masked_floor), axis=-1)
    weights = jnp.where(live_mask, jnp.exp(scores - local_max[..., None]), 0.0)
    local_sum = jnp.sum(weights, axis=-1)
    local_acc = jnp.einsum(
        "bhgt,bhtd->bhgd",
        weights.astype(jnp.bfloat16),
        stored_value_cache,
        preferred_element_type=jnp.float32,
    )
    merged_max, merged_sum, merged_acc = joined(
        (local_max, local_sum, local_acc), "seq", join_partial
    )
    score_new = (
        jnp.einsum(
            "bhgd,bhd->bhg", grouped_queries.astype(jnp.float32), fresh_key_rows.astype(jnp.float32)
        )
        * score_scale
    )
    row_max = jnp.maximum(merged_max, score_new)
    old_factor = jnp.exp(merged_max - row_max)
    new_weight = jnp.exp(score_new - row_max)
    total_weight = merged_sum * old_factor + new_weight
    attended = (
        merged_acc * old_factor[..., None]
        + new_weight[..., None] * fresh_value_rows.astype(jnp.float32)[:, :, None, :]
    )
    attn_rows = (
        (attended / total_weight[..., None])
        .reshape(batch_rows, q_local * head_dim)
        .astype(jnp.bfloat16)
    )
    out_part = jnp.dot(attn_rows, w_attn_out, preferred_element_type=jnp.float32)
    summed = lax.psum(out_part, "head")
    mid_stream = (token_float + summed).astype(jnp.bfloat16)
    full_tokens = lax.all_gather(mid_stream, "seq", axis=1, tiled=True)
    full_float = full_tokens.astype(jnp.float32)
    inv_rms_two = lax.rsqrt(jnp.mean(full_float * full_float, axis=1) + norm_eps)
    lifted_two = (full_float * inv_rms_two[:, None] * mamba_gain[None, :]).astype(jnp.bfloat16)
    inner = jnp.dot(lifted_two, w_in[0], preferred_element_type=jnp.float32)
    gate_branch = jnp.dot(lifted_two, w_in[1], preferred_element_type=jnp.float32)
    window = jnp.concatenate([conv_state, inner[:, None, :]], axis=1)
    mixed = jnp.sum(window * conv_weight[None, :, :], axis=1) + conv_bias[None, :]
    activated = jax.nn.silu(mixed)
    proj_part = jnp.dot(activated.astype(jnp.bfloat16), w_xproj, preferred_element_type=jnp.float32)
    projected = lax.psum(proj_part, ("seq", "head"))
    rank_width = w_dt.shape[0]
    state_width = ssm_state.shape[1]
    dt_low = projected[:, :rank_width].astype(jnp.bfloat16)
    input_map = projected[:, rank_width : rank_width + state_width]
    output_map = projected[:, rank_width + state_width :]
    step_size = jax.nn.softplus(
        jnp.dot(dt_low, w_dt, preferred_element_type=jnp.float32) + dt_bias[None, :]
    )
    decay = jnp.exp(step_size[:, None, :] * (-jnp.exp(a_log))[None, :, :])
    new_state = decay * ssm_state + (step_size * activated)[:, None, :] * input_map[:, :, None]
    readout = jnp.sum(output_map[:, :, None] * new_state, axis=1) + skip_gain[None, :] * activated
    gated = (readout * jax.nn.silu(gate_branch)).astype(jnp.bfloat16)
    mamba_part = jnp.dot(gated, w_mamba_out, preferred_element_type=jnp.float32)
    share = lax.psum_scatter(
        mamba_part.astype(jnp.bfloat16), "seq", scatter_dimension=1, tiled=True
    ).astype(jnp.float32)
    share = lax.psum(share, "head")
    hidden_out = (mid_stream.astype(jnp.float32) + share).astype(jnp.bfloat16)
    return (hidden_out, new_state)


def solution(mesh):
    in_specs = (
        P(("rep", "sub"), "seq"),
        P("seq"),
        P("seq", "head"),
        P("seq", "head"),
        P("seq", "head"),
        P("head", "seq"),
        P(("rep", "sub"), "head", "seq", None),
        P(("rep", "sub"), "head", "seq", None),
        P(("rep", "sub")),
        P(("rep", "sub")),
        P(),
        P(None, None, ("seq", "head")),
        P(None, ("seq", "head")),
        P(("seq", "head")),
        P(("rep", "sub"), None, ("seq", "head")),
        P(("seq", "head"), None),
        P(None, ("seq", "head")),
        P(("seq", "head")),
        P(None, ("seq", "head")),
        P(("seq", "head")),
        P(("rep", "sub"), None, ("seq", "head")),
        P(("seq", "head"), None),
    )
    out_specs = (P(("rep", "sub"), "seq"), P(("rep", "sub"), None, ("seq", "head")))
    return jax.shard_map(local, mesh=mesh, in_specs=in_specs, out_specs=out_specs, check_vma=False)
```

profile of v0, /device:TPU:0, one launch (start us, length us, event | category | flops | bytes accessed | tf_op | source)
XLA Modules:
  0.0 205.1 jit_solution(17046458614477309599)
XLA Ops:
  7.3 3.6 %fusion.46 = f32[8,2048]{1,0:T(8,128)} fusion(bf16[1024,2048]{1,0:T(8,128)(2,1)} %param.26, bf16[8,1024]{1,0:T(8,128)(2,1)} %param.24, f32[1024]{0:T(1024)} %param.25), kind=kOutput, calls=%fused_computation.68 | convolution fusion | flops 33579008 | bytes 4280320 | tf_op jit(solution)/shard_map/dot_general | solution.py:87
  11.0 0.1 fusion.25
  11.2 0.2 fusion.44
  11.4 0.2 fusion.42
  11.7 21.4 %all-reduce = (f32[8]{0:T(128)S(1)}, f32[8,512]{1,0:T(8,128)S(1)}, f32[8,512]{1,0:T(8,128)S(1)}) all-reduce(f32[8]{0:T(128)S(1)} %fusion.25, f32[8,512]{1,0:T(8,128)S(1)} %fusion.44, f32[8,512]{1,0:T(8,128)S(1)} %fusion.42), channel_id=1, replica_groups=mesh['rep'=2,'seq'=4,'head'=2,'sub'=2] {'seq'}, use_global_device_ids=true, to_apply=%region_2.0 | all-reduce | flops 8200 | bytes 65600 | tf_op jit(solution)/shard_map/psum | solution.py:91
  33.3 0.1 multiply_cosine_fusion
  33.6 14.7 %all-reduce.3.cloned.1.call-done = f32[8,2048]{1,0:T(8,128)} async-done(((f32[8,2048]{1,0:T(8,128)}), f32[8,2048]{1,0:T(8,128)}) %all-reduce.3.cloned.1.call-update) | async-done | bytes 65552 | tf_op jit(solution)/shard_map/psum | solution.py:92
  48.3 1.1 multiply_bitcast_fusion
  49.4 0.1 subtract_convert_fusion
  49.5 3.6 %select_reduce_fusion = (f32[8,4,4]{2,1,0:T(4,128)S(1)}, f32[8,4,4,512]{3,2,1,0:T(4,128)S(1)}) fusion(pred[8,512]{1,0:T(8,128)(4,1)S(1)} %broadcast_compare_fusion, bf16[8,4,512,128]{3,2,1,0:T(8,128)(2,1)} %param.30, bf16[8,4,4,64]{3,2,1,0:T(4,128)(2,1)S(1)} %bitcast.72, bf16[8,4,4,64]{3,2,1,0:T(4,128)(2,1)S(1)} %bitcast.70), kind=kOutput, calls=%fused_computation.21 | convolution fusion | flops 17039232 | bytes 4493824 | tf_op jit(solution)/shard_map/bhgd,bhtd->bhgt/dot_general | solution.py:106
  53.1 13.1 %all-gather = f32[32,4,4]{2,1,0:T(4,128)S(1)} all-gather(f32[8,4,4]{2,1,0:T(4,128)S(1)} %get-tuple-element.94), channel_id=2, replica_groups=mesh['rep'=2,'seq'=4,'head'=2,'sub'=2] {'seq'}, dimensions={0}, use_global_device_ids=true | all-gather | bytes 2560 | tf_op jit(solution)/shard_map/all_gather | solution.py:14
  66.2 0.3 fusion.13
  66.5 13.2 %all-gather.1 = f32[32,4,4]{2,1,0:T(4,128)S(1)} all-gather(f32[8,4,4]{2,1,0:T(4,128)S(1)} %fusion.13), channel_id=3, replica_groups=mesh['rep'=2,'seq'=4,'head'=2,'sub'=2] {'seq'}, dimensions={0}, use_global_device_ids=true | all-gather | bytes 2560 | tf_op jit(solution)/shard_map/all_gather | solution.py:14
  79.7 0.7 fusion.17
  80.4 13.9 %all-gather.2 = f32[32,4,4,128]{3,2,1,0:T(4,128)S(1)} all-gather(f32[8,4,4,128]{3,2,1,0:T(4,128)S(1)} %fusion.17), channel_id=4, replica_groups=mesh['rep'=2,'seq'=4,'head'=2,'sub'=2] {'seq'}, dimensions={0}, use_global_device_ids=true | all-gather | bytes 327680 | tf_op jit(solution)/shard_map/all_gather | solution.py:14
  94.3 0.2 fusion.37
  94.6 0.1 copy.59
  94.7 0.1 copy.50
  94.8 0.2 copy.52
  94.9 0.1 copy.51
  95.0 0.2 copy.53
  95.2 1.5 while.14
  95.2 0.1 copy.68
  95.3 0.1 copy.69
  95.4 0.2 fusion.73
  95.7 0.1 copy.68
  95.8 0.1 copy.69
  95.9 0.2 fusion.73
  96.2 0.1 copy.68
  96.3 0.1 copy.69
  96.4 0.2 fusion.73
  96.7 0.1 copy.57
  96.8 0.1 copy.54
  96.9 0.1 copy.55
  97.0 0.2 fusion.23
  97.2 2.8 %fusion.59 = f32[8,1024]{1,0:T(8,128)S(1)} fusion(bf16[8,2048]{1,0:T(8,128)(2,1)S(1)} %convert_element_type.78, bf16[2048,1024]{1,0:T(8,128)(2,1)} %param.29), kind=kOutput, calls=%fused_computation.88 | convolution fusion | flops 33554432 | bytes 4259840 | tf_op jit(solution)/shard_map/dot_general | solution.py:144
  100.0 8.3 %psum.53 = f32[8,1024]{1,0:T(8,128)S(1)} all-reduce(f32[8,1024]{1,0:T(8,128)S(1)} %fusion.59), channel_id=1, replica_groups=mesh['rep'=2,'seq'=4,'head'=2,'sub'=2] {'head'}, use_global_device_ids=true, to_apply=%region_9.10 | all-reduce | flops 8192 | bytes 65536 | tf_op jit(solution)/shard_map/psum | solution.py:145
  108.4 13.1 %all_gather.27 = bf16[8,4096]{1,0:T(8,128)(2,1)S(1)} all-gather(bf16[8,1024]{1,0:T(8,128)(2,1)S(1)} %fusion.26), channel_id=1, replica_groups=mesh['rep'=2,'seq'=4,'head'=2,'sub'=2] {'seq'}, dimensions={1}, use_global_device_ids=true | all-gather | bytes 81920 | tf_op jit(solution)/shard_map/all_gather | solution.py:147
  121.5 0.1 fusion.14
  121.8 4.7 %fusion.9 = f32[8,1,1024]{2,0,1:T(8,128)S(1)} fusion(bf16[2,4096,1024]{2,1,0:T(8,128)(2,1)} %param.35, bf16[8,4096]{1,0:T(8,128)(2,1)S(1)} %all_gather.27, f32[4096]{0:T(1024)S(1)} %copy-done.9, f32[8]{0:T(128)S(1)} %add_rsqrt_fusion), kind=kOutput, calls=%fused_computation.16 | convolution fusion | flops 67239936 | bytes 8503328 | tf_op jit(solution)/shard_map/dot_general | solution.py:151
  126.5 0.3 fusion.34
  126.8 35.1 %psum.54 = f32[8,288]{1,0:T(8,128)S(1)} all-reduce(f32[8,288]{1,0:T(8,128)S(1)} %fusion.34), channel_id=1, replica_groups=mesh['rep'=2,'seq'=4,'head'=2,'sub'=2] {'seq','head'}, use_global_device_ids=true, to_apply=%region_12.13 | all-reduce | flops 2304 | bytes 18432 | tf_op jit(solution)/shard_map/psum | solution.py:157
  162.0 0.2 fusion.54
  162.2 1.0 multiply_reduce_fusion
  163.2 8.7 %convolution_convert_fusion = bf16[8,4096]{1,0:T(8,128)(2,1)} fusion(bf16[1024,4096]{1,0:T(8,128)(2,1)} %param.45, bf16[2,4096,1024]{2,1,0:T(8,128)(2,1)} %param.35, f32[8,1024]{1,0:T(8,128)S(1)} %get-tuple-element.79, f32[1024]{0:T(1024)S(1)} %copy-done.14, bf16[8,4096]{1,0:T(8,128)(2,1)S(1)} %all_gather.27, f32[4096]{0:T(1024)S(1)} %copy-done.9, ...), kind=kOutput, calls=%fused_computation.14 | convolution fusion | flops 134488064 | bytes 16998432 | tf_op jit(solution)/shard_map/dot_general | solution.py:170
  172.0 16.6 %reduce-scatter.2.cloned.1.call-done = bf16[8,1024]{1,0:T(8,128)(2,1)} async-done(((bf16[8,4096]{1,0:T(8,128)(2,1)}), bf16[8,1024]{1,0:T(8,128)(2,1)}) %reduce-scatter.2.cloned.1.call-update) | async-done | bytes 16400 | tf_op jit(solution)/shard_map/reduce_scatter | solution.py:171
  188.6 9.0 %psum.55 = f32[8,1024]{1,0:T(8,128)S(1)} all-reduce(bf16[8,1024]{1,0:T(8,128)(2,1)} %reduce-scatter.2.cloned.1.call-done), channel_id=1, replica_groups=mesh['rep'=2,'seq'=4,'head'=2,'sub'=2] {'head'}, use_global_device_ids=true, to_apply=%region_15.16 | all-reduce | flops 8192 | bytes 49152 | tf_op jit(solution)/shard_map/psum | solution.py:174
  197.6 0.6 add_convert_fusion.1
  (65 shorter events, 0.9 us)
Async XLA Ops:
  7.2 4.0 %copy-start = (bf16[1024,512]{1,0:T(8,128)(2,1)S(1)}, bf16[1024,512]{1,0:T(8,128)(2,1)}, u32[]{:S(2)}) copy-start(bf16[1024,512]{1,0:T(8,128)(2,1)} %param.27) | copy-start | bytes 3145732
  7.2 3.8 %copy-start.6 = (bf16[8,1024]{1,0:T(8,128)(2,1)S(1)}, bf16[8,1024]{1,0:T(8,128)(2,1)}, u32[]{:S(2)}) copy-start(bf16[8,1024]{1,0:T(8,128)(2,1)} %param.24) | copy-start | bytes 49156
  7.2 4.0 %copy-start.10 = (f32[1024]{0:T(1024)S(1)}, f32[1024]{0:T(1024)}, u32[]{:S(2)}) copy-start(f32[1024]{0:T(1024)} %param.25) | copy-start | bytes 12292
  7.2 4.2 %copy-start.2 = (bf16[1024,512]{1,0:T(8,128)(2,1)S(1)}, bf16[1024,512]{1,0:T(8,128)(2,1)}, u32[]{:S(2)}) copy-start(bf16[1024,512]{1,0:T(8,128)(2,1)} %param.28) | copy-start | bytes 3145732
  7.2 4.5 %copy-start.16 = (s32[8]{0:T(128)S(1)}, s32[8]{0:T(128)}, u32[]{:S(2)}) copy-start(s32[8]{0:T(128)} %param.33) | copy-start | bytes 100
  7.2 26.0 %copy-start.8 = (f32[16,1024]{1,0:T(8,128)S(1)}, f32[16,1024]{1,0:T(8,128)}, u32[]{:S(2)}) copy-start(f32[16,1024]{1,0:T(8,128)} %param.42) | copy-start | bytes 196612
  7.2 26.0 %copy-start.15 = (s32[8]{0:T(128)S(1)}, s32[8]{0:T(128)}, u32[]{:S(2)}) copy-start(s32[8]{0:T(128)} %param.32) | copy-start | bytes 100
  7.2 41.0 %all-reduce.3.cloned.1.call-start = ((), (), s32[]{:S(2)}) async-start(), calls=%async_computation.1 | async-start | bytes 131072 | tf_op jit(solution)/shard_map/psum | solution.py:92
  11.0 177.7 %reduce-scatter.2.cloned.1.call-start = ((), (), s32[]{:S(2)}) async-start(), calls=%async_computation.2 | async-start | bytes 81920 | tf_op jit(solution)/shard_map/reduce_scatter | solution.py:171
  48.3 31.4 %copy-start.1 = (bf16[8,4,512,128]{3,2,1,0:T(8,128)(2,1)S(1)}, bf16[8,4,512,128]{3,2,1,0:T(8,128)(2,1)}, u32[]{:S(2)}) copy-start(bf16[8,4,512,128]{3,2,1,0:T(8,128)(2,1)} %param.31) | copy-start | bytes 12582916
  80.4 41.3 %copy-start.9 = (f32[4096]{0:T(1024)S(1)}, f32[4096]{0:T(1024)}, u32[]{:S(2)}) copy-start(f32[4096]{0:T(1024)} %param.34) | copy-start | bytes 49156
  121.7 4.8 %copy-start.7 = (f32[8,3,1024]{2,0,1:T(8,128)S(1)}, f32[8,3,1024]{2,0,1:T(8,128)}, u32[]{:S(2)}) copy-start(f32[8,3,1024]{2,0,1:T(8,128)} %param.38) | copy-start | bytes 294916
  121.7 4.8 %copy-start.12 = (f32[4,1024]{1,0:T(4,128)S(1)}, f32[4,1024]{1,0:T(4,128)}, u32[]{:S(2)}) copy-start(f32[4,1024]{1,0:T(4,128)} %param.36) | copy-start | bytes 49156
  121.7 4.8 %copy-start.3 = (bf16[1024,288]{0,1:T(8,128)(2,1)S(1)}, bf16[1024,288]{0,1:T(8,128)(2,1)}, u32[]{:S(2)}) copy-start(bf16[1024,288]{0,1:T(8,128)(2,1)} %param.39) | copy-start | bytes 1769476
  121.7 4.8 %copy-start.11 = (f32[1024]{0:T(1024)S(1)}, f32[1024]{0:T(1024)}, u32[]{:S(2)}) copy-start(f32[1024]{0:T(1024)} %param.37) | copy-start | bytes 12292
  121.7 40.2 %copy-start.5 = (bf16[256,1024]{1,0:T(8,128)(2,1)S(1)}, bf16[256,1024]{1,0:T(8,128)(2,1)}, u32[]{:S(2)}) copy-start(bf16[256,1024]{1,0:T(8,128)(2,1)} %param.40) | copy-start | bytes 1572868
  121.7 40.2 %copy-start.13 = (f32[1024]{0:T(1024)S(1)}, f32[1024]{0:T(1024)}, u32[]{:S(2)}) copy-start(f32[1024]{0:T(1024)} %param.41) | copy-start | bytes 12292
  121.7 40.4 %copy-start.4 = (f32[8,16,1024]{2,1,0:T(8,128)S(1)}, f32[8,16,1024]{2,1,0:T(8,128)}, u32[]{:S(2)}) copy-start(f32[8,16,1024]{2,1,0:T(8,128)} %param.44) | copy-start | bytes 1572868
  121.8 41.5 %copy-start.14 = (f32[1024]{0:T(1024)S(1)}, f32[1024]{0:T(1024)}, u32[]{:S(2)}) copy-start(f32[1024]{0:T(1024)} %param.43) | copy-start | bytes 12292
Sparse Core Ops, SparseCore 0:
  11.1 37.1 all-reduce.2
  172.1 16.4 reduce-scatter.1
where the time goes:
time: 205 us
  blocking collectives  127 us (62%)
  waiting for transfers between devices  31.3 us (15%)
  matrix products  25.4 us (12%)
  between operations  14.4 us (7%)
  other arithmetic  4.82 us (2%)
    all_gather x3, blocking collectives, joined(): pieces = jax.tree.map(lambda part: lax.all_gather(part, axis), value)  40.2 us
    psum x1, blocking collectives, local(): projected = lax.psum(proj_part, ('seq', 'head'))  35.1 us
    psum x1, blocking collectives, local(): sum_squares = lax.psum(squares, 'seq')  21.4 us
    reduce_scatter x1, waiting for transfers between devices, local(): lax.psum_scatter(mamba_part.astype(jnp.bfloat16), 'seq', scatter_dimensio...  16.6 us
    psum x1, waiting for transfers between devices, local(): lax.psum((part_query, part_key, part_value), 'seq')  14.7 us
    all_gather x1, blocking collectives, local(): full_tokens = lax.all_gather(mid_stream, 'seq', axis=1, tiled=True)  13.1 us
    psum x1, blocking collectives, local(): share = lax.psum(share, 'head')  8.99 us
    dot_general x1, matrix products, local(): mamba_part = jnp.dot(gated, w_mamba_out, preferred_element_type=jnp.float32)  8.73 us
  transfers between devices with their start and end apart: 2, of which 2 were waited for; matrix products, arithmetic and copies ran while one was open for 1% of the time, Pallas kernels for 0%

commit v1 on v0

--- a/solution.py
+++ b/solution.py
@@ -1,8 +1,11 @@
+import functools
 import math
 
 import jax
 import jax.numpy as jnp
 from jax import lax
+from jax.experimental import pallas as pl
+from jax.experimental.pallas import tpu as pltpu
 from jax.sharding import PartitionSpec as P
 
 norm_eps = 1e-05
@@ -176,6 +179,579 @@
     return (hidden_out, new_state)
 
 
+MESH = pl.DeviceIdType.MESH
+
+
+def farthest_first(count):
+    return sorted(range(1, count), key=lambda k: -min(k, count - k))
+
+
+def rotate(vectors, cosine, sine_signed):
+    half_dim = vectors.shape[-1] // 2
+    return vectors * cosine + pltpu.roll(vectors, half_dim, 1) * sine_signed
+
+
+def fused_kernel(
+    seq_count,
+    head_count,
+    length_ref,
+    position_ref,
+    token_ref,
+    attn_gain_ref,
+    mamba_gain_ref,
+    conv_weight_ref,
+    conv_bias_ref,
+    dt_bias_ref,
+    a_log_ref,
+    skip_gain_ref,
+    wq_hbm,
+    wk_hbm,
+    wv_hbm,
+    wo_hbm,
+    ck_hbm,
+    cv_hbm,
+    win_hbm,
+    cs_hbm,
+    wx_hbm,
+    wdt_hbm,
+    state_hbm,
+    wm_hbm,
+    hidden_ref,
+    new_state_hbm,
+    wq,
+    wk,
+    wv,
+    wo,
+    ck,
+    cv,
+    win,
+    cs,
+    wx,
+    wdt,
+    state,
+    wm,
+    new_state,
+    load_sem,
+    q_part,
+    kv_part,
+    ssq_part,
+    q_slots,
+    kv_slots,
+    ssq_slots,
+    q_rows,
+    scores,
+    acc_rows,
+    ml_rows,
+    acc_part,
+    ml_part,
+    acc_slots,
+    ml_slots,
+    attn_x,
+    out_part,
+    out_slots,
+    mid_part,
+    mid_slots,
+    gains,
+    inner_acc,
+    proj_part,
+    proj_slots,
+    y_rows,
+    gated_x,
+    share_part,
+    share_slots,
+    seq_send,
+    seq_recv,
+    head_send,
+    head_recv,
+    all_send,
+    all_recv,
+):
+    rows, feature = token_ref.shape
+    head_dim = ck.shape[3]
+    kv_local = ck.shape[1]
+    ctx = ck.shape[2]
+    q_cols = wq.shape[1]
+    kv_cols = wk.shape[1]
+    q_heads = q_cols // head_dim
+    group = q_heads // kv_local
+    model = feature * seq_count
+    chan = wm.shape[0]
+    nstate = a_log_ref.shape[0]
+    rank = wdt.shape[0]
+    f32 = jnp.float32
+    bf16 = jnp.bfloat16
+    my_seq = lax.axis_index("seq")
+    my_head = lax.axis_index("head")
+
+    def peer(ks, kh):
+        return {
+            "seq": lax.rem(my_seq + ks, seq_count),
+            "head": lax.rem(my_head + kh, head_count),
+        }
+
+    loads = []
+    for src, dst in (
+        (wq_hbm, wq),
+        (wk_hbm, wk),
+        (wv_hbm, wv),
+        (ck_hbm, ck),
+        (cv_hbm, cv),
+        (wo_hbm, wo),
+        (win_hbm, win),
+        (cs_hbm, cs),
+        (wx_hbm, wx),
+        (wdt_hbm, wdt),
+        (state_hbm, state),
+        (wm_hbm, wm),
+    ):
+        copy = pltpu.make_async_copy(src, dst, load_sem.at[len(loads)])
+        copy.start()
+        loads.append(copy)
+    (ld_wq, ld_wk, ld_wv, ld_ck, ld_cv, ld_wo, ld_win, ld_cs, ld_wx, ld_wdt, ld_state, ld_wm) = loads
+
+    barrier = pltpu.get_barrier_semaphore()
+    everyone = [
+        (ks, kh) for ks in range(seq_count) for kh in range(head_count) if ks or kh
+    ]
+    everyone.sort(key=lambda o: -(min(o[0], seq_count - o[0]) + min(o[1], head_count - o[1])))
+    for ks, kh in everyone:
+        pl.semaphore_signal(barrier, inc=1, device_id=peer(ks, kh), device_id_type=MESH)
+
+    seq_order = farthest_first(seq_count)
+    near_order = seq_order[::-1]
+    pending = []
+
+    def seq_push(phase, src, slots):
+        for k in seq_order:
+            copy = pltpu.make_async_remote_copy(
+                src_ref=src,
+                dst_ref=slots.at[k],
+                send_sem=seq_send.at[phase, k],
+                recv_sem=seq_recv.at[phase, k],
+                device_id=peer(k, 0),
+                device_id_type=MESH,
+            )
+            copy.start()
+            pending.append(copy)
+
+    def seq_wait(phase, k, src, slots):
+        pltpu.make_async_remote_copy(
+            src_ref=src,
+            dst_ref=slots.at[k],
+            send_sem=seq_send.at[phase, k],
+            recv_sem=seq_recv.at[phase, k],
+            device_id=peer(k, 0),
+            device_id_type=MESH,
+        ).wait_recv()
+
+    token_float = token_ref[...].astype(f32)
+    lifted = (token_float * attn_gain_ref[...][None, :]).astype(bf16)
+    squares = jnp.sum(token_float * token_float, axis=1, keepdims=True)
+    ssq_part[...] = jnp.broadcast_to(squares, ssq_part.shape)
+
+    half_dim = head_dim // 2
+    lane = lax.broadcasted_iota(jnp.int32, (rows, head_dim), 1)
+    frequency = jnp.exp(
+        -math.log(rope_base) * 2.0 * (lane % half_dim).astype(f32) / (2 * half_dim)
+    )
+    row_index = lax.broadcasted_iota(jnp.int32, (rows, head_dim), 0)
+    position = jnp.zeros((rows, head_dim), f32)
+    for b in range(rows):
+        position = jnp.where(row_index == b, position_ref[b].astype(f32), position)
+    angles = position * frequency
+    cosine = jnp.cos(angles)
+    sine_signed = jnp.where(lane < half_dim, -jnp.sin(angles), jnp.sin(angles))
+    mg = mamba_gain_ref[...]
+    for s in range(seq_count):
+        gains[s] = jnp.broadcast_to(mg[s * feature : (s + 1) * feature][None, :], (rows, feature))
+
+    tile = 512
+
+    def dot(a, b):
+        return jnp.dot(a, b, preferred_element_type=f32)
+
+    ld_wq.wait()
+    for n in range(0, q_cols, tile):
+        q_part[:, n : n + tile] = dot(lifted, wq[:, n : n + tile]).astype(bf16)
+    pl.semaphore_wait(barrier, len(everyone))
+    seq_push(0, ssq_part, ssq_slots)
+    seq_push(1, q_part, q_slots)
+    ld_wk.wait()
+    kv_part[:, :kv_cols] = dot(lifted, wk[...]).astype(bf16)
+    ld_wv.wait()
+    kv_part[:, kv_cols:] = dot(lifted, wv[...]).astype(bf16)
+    seq_push(2, kv_part, kv_slots)
+
+    for k in near_order:
+        seq_wait(0, k, ssq_part, ssq_slots)
+        seq_wait(1, k, q_part, q_slots)
+    ssq = ssq_part[...]
+    for k in near_order:
+        ssq = ssq + ssq_slots[k]
+    inv_rms = lax.rsqrt(ssq / model + norm_eps)
+    for j in range(q_heads):
+        cols = slice(j * head_dim, (j + 1) * head_dim)
+        total = q_part[:, cols].astype(f32)
+        for k in near_order:
+            total = total + q_slots[k, :, cols].astype(f32)
+        spun = rotate(total * inv_rms, cosine, sine_signed)
+        q_rows[j * rows : (j + 1) * rows, :] = spun.astype(bf16).astype(f32)
+
+    score_scale = head_dim ** (-0.5)
+    pair_rows = 2 * group
+    pair_stride = pair_rows * rows
+    upper = lax.broadcasted_iota(jnp.int32, (pair_rows, head_dim), 0) < group
+    slot_index = my_seq * ctx + lax.broadcasted_iota(jnp.int32, (pair_rows, ctx), 1)
+    pairs = [(b, p) for b in range(rows) for p in range(kv_local // 2)]
+    ld_ck.wait()
+    for index, (b, p) in enumerate(pairs):
+        x = q_rows[pl.ds(p * pair_stride + b, pair_rows, stride=rows), :]
+        left = jnp.concatenate([jnp.where(upper, x, 0.0), jnp.where(upper, 0.0, x)], axis=1)
+        keys = jnp.concatenate([ck[b, 2 * p], ck[b, 2 * p + 1]], axis=1)
+        scores[index] = lax.dot_general(
+            left.astype(bf16), keys, (((1,), (1,)), ((), ())), preferred_element_type=f32
+        )
+    ld_cv.wait()
+    lane_row = lax.broadcasted_iota(jnp.int32, (pair_rows, head_dim), 1)
+    for index, (b, p) in enumerate(pairs):
+        live = slot_index < length_ref[b]
+        s = jnp.where(live, scores[index] * score_scale, masked_floor)
+        top = jnp.max(s, axis=1, keepdims=True)
+        w = jnp.where(live, jnp.exp(s - top), 0.0)
+        sum_w = jnp.sum(w, axis=1, keepdims=True)
+        values = jnp.concatenate([cv[b, 2 * p], cv[b, 2 * p + 1]], axis=1)
+        both = dot(w.astype(bf16), values)
+        acc = jnp.where(upper, both[:, :head_dim], both[:, head_dim:])
+        acc = acc / jnp.maximum(sum_w, 1e-30)
+        spot = pl.ds(p * pair_stride + b, pair_rows, stride=rows)
+        acc_rows[spot, :] = acc
+        ml_rows[spot, :] = jnp.where(lane_row < half_dim, top, sum_w)
+    acc_part[...] = acc_rows[...].astype(bf16)
+    n_rows = q_heads * rows
+    diag = lax.broadcasted_iota(jnp.int32, (n_rows, n_rows), 0) == lax.broadcasted_iota(
+        jnp.int32, (n_rows, n_rows), 1
+    )
+
+    def to_lanes(column):
+        return jnp.sum(jnp.where(diag, column, 0.0), axis=0, keepdims=True)
+
+    def to_rows(line):
+        return jnp.sum(jnp.where(diag, line, 0.0), axis=1, keepdims=True)
+
+    ml = ml_rows[...]
+    ml_part[0:1, :] = to_lanes(ml[:, 0:1])
+    ml_part[1:2, :] = to_lanes(ml[:, half_dim : half_dim + 1])
+    ml_part[2:8, :] = jnp.zeros((6, n_rows), f32)
+    seq_push(3, ml_part, ml_slots)
+    seq_push(4, acc_part, acc_slots)
+
+    for k in near_order:
+        seq_wait(2, k, kv_part, kv_slots)
+
+    def joined_kv(cols):
+        total = kv_part[:, cols].astype(f32)
+        for k in near_order:
+            total = total + kv_slots[k, :, cols].astype(f32)
+        return total * inv_rms
+
+    new_scores = []
+    new_values = []
+    for h in range(kv_local):
+        key = rotate(joined_kv(slice(h * head_dim, (h + 1) * head_dim)), cosine, sine_signed)
+        key = key.astype(bf16).astype(f32)
+        new_values.append(
+            joined_kv(slice(kv_cols + h * head_dim, kv_cols + (h + 1) * head_dim))
+            .astype(bf16)
+            .astype(f32)
+        )
+        for g in range(group):
+            j = h * group + g
+            q = q_rows[j * rows : (j + 1) * rows, :]
+            new_scores.append(jnp.sum(q * key, axis=1, keepdims=True) * score_scale)
+    score_new = to_lanes(jnp.concatenate(new_scores, axis=0))
+
+    for k in near_order:
+        seq_wait(3, k, ml_part, ml_slots)
+    stats = [(ml_part[0:1, :], ml_part[1:2, :])]
+    stats += [(ml_slots[k, 0:1, :], ml_slots[k, 1:2, :]) for k in near_order]
+    row_max = score_new
+    for m_one, _ in stats:
+        row_max = jnp.maximum(row_max, m_one)
+    shares = [jnp.exp(m_one - row_max) * l_one for m_one, l_one in stats]
+    new_weight = jnp.exp(score_new - row_max)
+    total_weight = new_weight
+    for one in shares:
+        total_weight = total_weight + one
+    factors = [to_rows(one / total_weight) for one in shares]
+    new_factor = to_rows(new_weight / total_weight)
+    for k in near_order:
+        seq_wait(4, k, acc_part, acc_slots)
+    for j in range(q_heads):
+        at = slice(j * rows, (j + 1) * rows)
+        merged = acc_rows[at, :] * factors[0][at] + new_factor[at] * new_values[j // group]
+        for i, k in enumerate(near_order):
+            merged = merged + acc_slots[k, at, :].astype(f32) * factors[1 + i][at]
+        attn_x[:, j * head_dim : (j + 1) * head_dim] = merged.astype(bf16)
+
+    ld_wo.wait()
+    x = attn_x[...]
+    for n in range(0, feature, tile):
+        out_part[:, n : n + tile] = dot(x, wo[:, n : n + tile])
+    for k in range(1, head_count):
+        copy = pltpu.make_async_remote_copy(
+            src_ref=out_part,
+            dst_ref=out_slots.at[k],
+            send_sem=head_send.at[k],
+            recv_sem=head_recv.at[k],
+            device_id=peer(0, k),
+            device_id_type=MESH,
+        )
+        copy.start()
+        pending.append(copy)
+    for k in range(1, head_count):
+        pltpu.make_async_remote_copy(
+            src_ref=out_part,
+            dst_ref=out_slots.at[k],
+            send_sem=head_send.at[k],
+            recv_sem=head_recv.at[k],
+            device_id=peer(0, k),
+            device_id_type=MESH,
+        ).wait_recv()
+    summed = out_part[...]
+    for k in range(1, head_count):
+        summed = summed + out_slots[k]
+    mid = (token_float + summed).astype(bf16)
+    mid_part[...] = mid
+    seq_push(5, mid_part, mid_slots)
+
+    ld_win.wait()
+    ssq_b = jnp.zeros((rows, 1), f32)
+    for k in [0] + near_order:
+        if k:
+            seq_wait(5, k, mid_part, mid_slots)
+            block = mid_slots[k].astype(f32)
+        else:
+            block = mid.astype(f32)
+        owner = lax.rem(my_seq - k + seq_count, seq_count)
+        ssq_b = ssq_b + jnp.sum(block * block, axis=1, keepdims=True)
+        x = (block * gains[owner]).astype(bf16)
+        at = pl.ds(pl.multiple_of(owner * feature, feature), feature)
+        for i in range(2):
+            for n in range(0, chan, tile):
+                cols = slice(n, min(n + tile, chan))
+                part = dot(x, win[i, at, cols])
+                if k:
+                    part = part + inner_acc[i, :, cols]
+                inner_acc[i, :, cols] = part
+    inv_b = lax.rsqrt(ssq_b / model + norm_eps)
+    inner = inner_acc[0] * inv_b
+    ld_cs.wait()
+    taps = conv_weight_ref.shape[0]
+    mixed = inner * conv_weight_ref[taps - 1 : taps, :] + conv_bias_ref[...][None, :]
+    for k in range(taps - 1):
+        mixed = mixed + cs[:, k, :] * conv_weight_ref[k : k + 1, :]
+    u = mixed / (1.0 + jnp.exp(-mixed))
+    ld_wx.wait()
+    proj_width = wx.shape[1]
+    proj_part[...] = jnp.zeros(proj_part.shape, f32)
+    proj_part[:, :proj_width] = dot(u.astype(bf16), wx[...])
+    order = list(enumerate(everyone))
+
+    def all_copy(phase, index, ks, kh, src, slots):
+        return pltpu.make_async_remote_copy(
+            src_ref=src,
+            dst_ref=slots.at[index],
+            send_sem=all_send.at[phase, index],
+            recv_sem=all_recv.at[phase, index],
+            device_id=peer(ks, kh),
+            device_id_type=MESH,
+        )
+
+    for index, (ks, kh) in order:
+        copy = all_copy(0, index, ks, kh, proj_part, proj_slots)
+        copy.start()
+        pending.append(copy)
+    gate = inner_acc[1] * inv_b
+    gate_silu = gate / (1.0 + jnp.exp(-gate))
+    decay_rate = -jnp.exp(a_log_ref[...])
+    ld_wdt.wait()
+    ld_state.wait()
+    for index, (ks, kh) in order:
+        all_copy(0, index, ks, kh, proj_part, proj_slots).wait_recv()
+    projected = proj_part[...]
+    for index, _ in order:
+        projected = projected + proj_slots[index]
+    low = dot(projected[:, :rank].astype(bf16), wdt[...]) + dt_bias_ref[...][None, :]
+    dt = jnp.maximum(low, 0.0) + jnp.log1p(jnp.exp(-jnp.abs(low)))
+    dtu = dt * u
+    maps = projected[:, rank:]
+    map_lane = lax.broadcasted_iota(jnp.int32, (nstate, maps.shape[1]), 1)
+    map_row = lax.broadcasted_iota(jnp.int32, (nstate, maps.shape[1]), 0)
+    for b in range(rows):
+        line = maps[b : b + 1, :]
+        bm = jnp.sum(jnp.where(map_lane == map_row, line, 0.0), axis=1, keepdims=True)
+        cm = jnp.sum(jnp.where(map_lane == map_row + nstate, line, 0.0), axis=1, keepdims=True)
+        fresh = jnp.exp(dt[b : b + 1, :] * decay_rate) * state[b] + dtu[b : b + 1, :] * bm
+        new_state[b] = fresh
+        y_rows[b : b + 1, :] = jnp.sum(cm * fresh, axis=0, keepdims=True)
+    store = pltpu.make_async_copy(new_state, new_state_hbm, load_sem.at[len(loads)])
+    store.start()
+    readout = y_rows[...] + skip_gain_ref[...][None, :] * u
+    gated_x[...] = (readout * gate_silu).astype(bf16)
+
+    ld_wm.wait()
+    own = None
+    for ks in seq_order + [0]:
+        owner = lax.rem(my_seq + ks, seq_count)
+        x = gated_x[...]
+        for n in range(0, feature, tile):
+            at = pl.ds(pl.multiple_of(owner * feature + n, tile), tile)
+            share_part[ks, :, n : n + tile] = dot(x, wm[:, at]).astype(bf16)
+        for index, (ps, kh) in order:
+            if ps == ks:
+                copy = all_copy(1, index, ps, kh, share_part.at[ks], share_slots)
+                copy.start()
+                pending.append(copy)
+    total = share_part[0].astype(f32)
+    for index, (ps, kh) in order:
+        all_copy(1, index, ps, kh, share_part.at[ps], share_slots).wait_recv()
+    for index, _ in order:
+        total = total + share_slots[index].astype(f32)
+    hidden_ref[...] = (mid_part[...].astype(f32) + total).astype(bf16)
+    store.wait()
+    for copy in pending:
+        copy.wait_send()
+
+
+def fused(seq_count, head_count, *args):
+    (
+        tokens,
+        attn_gain,
+        w_query,
+        key_projection_weight,
+        value_projection_weight,
+        w_attn_out,
+        cache_keys,
+        stored_value_cache,
+        lengths,
+        positions,
+        mamba_gain,
+        w_in,
+        conv_weight,
+        conv_bias,
+        conv_state,
+        w_xproj,
+        w_dt,
+        dt_bias,
+        a_log,
+        skip_gain,
+        ssm_state,
+        w_mamba_out,
+    ) = args
+    rows, feature = tokens.shape
+    q_cols = w_query.shape[1]
+    kv_cols = key_projection_weight.shape[1]
+    head_dim = cache_keys.shape[3]
+    kv_local = cache_keys.shape[1]
+    ctx = cache_keys.shape[2]
+    q_heads = q_cols // head_dim
+    chan = w_mamba_out.shape[0]
+    n_rows = q_heads * rows
+    pair_rows = 2 * q_heads // kv_local
+    blocks = n_rows // pair_rows
+    proj_pad = -(-w_xproj.shape[1] // 128) * 128
+    others = seq_count * head_count - 1
+    f32 = jnp.float32
+    bf16 = jnp.bfloat16
+    big = (
+        w_query,
+        key_projection_weight,
+        value_projection_weight,
+        w_attn_out,
+        cache_keys,
+        stored_value_cache,
+        w_in,
+        conv_state,
+        w_xproj,
+        w_dt,
+        ssm_state,
+        w_mamba_out,
+    )
+    small = (tokens, attn_gain, mamba_gain, conv_weight, conv_bias, dt_bias, a_log, skip_gain)
+    V = pltpu.VMEM
+    dma = pltpu.SemaphoreType.DMA
+    scratch = [V(a.shape, a.dtype) for a in big] + [
+        V(ssm_state.shape, f32),
+        dma((len(big) + 1,)),
+        V((rows, q_cols), bf16),
+        V((rows, 2 * kv_cols), bf16),
+        V((rows, head_dim), f32),
+        V((seq_count, rows, q_cols), bf16),
+        V((seq_count, rows, 2 * kv_cols), bf16),
+        V((seq_count, rows, head_dim), f32),
+        V((n_rows, head_dim), f32),
+        V((blocks, pair_rows, ctx), f32),
+        V((n_rows, head_dim), f32),
+        V((n_rows, head_dim), f32),
+        V((n_rows, head_dim), bf16),
+        V((8, n_rows), f32),
+        V((seq_count, n_rows, head_dim), bf16),
+        V((seq_count, 8, n_rows), f32),
+        V((rows, q_cols), bf16),
+        V((rows, feature), f32),
+        V((head_count, rows, feature), f32),
+        V((rows, feature), bf16),
+        V((seq_count, rows, feature), bf16),
+        V((seq_count, rows, feature), f32),
+        V((2, rows, chan), f32),
+        V((rows, proj_pad), f32),
+        V((others, rows, proj_pad), f32),
+        V((rows, chan), f32),
+        V((rows, chan), bf16),
+        V((seq_count, rows, feature), bf16),
+        V((others, rows, feature), bf16),
+        dma((6, seq_count)),
+        dma((6, seq_count)),
+        dma((head_count,)),
+        dma((head_count,)),
+        dma((2, others)),
+        dma((2, others)),
+    ]
+    smem = pl.BlockSpec(memory_space=pltpu.SMEM)
+    vmem = pl.BlockSpec(memory_space=pltpu.VMEM)
+    hbm = pl.BlockSpec(memory_space=pl.ANY)
+    return pl.pallas_call(
+        functools.partial(fused_kernel, seq_count, head_count),
+        out_shape=(
+            jax.ShapeDtypeStruct((rows, feature), bf16),
+            jax.ShapeDtypeStruct(ssm_state.shape, f32),
+        ),
+        in_specs=[smem, smem] + [vmem] * len(small) + [hbm] * len(big),
+        out_specs=(vmem, hbm),
+        scratch_shapes=scratch,
+        compiler_params=pltpu.CompilerParams(
+            collective_id=0, has_side_effects=True, vmem_limit_bytes=60 * 1024 * 1024
+        ),
+    )(lengths, positions, *small, *big)
+
+
+def fits(mesh, args):
+    tokens, w_query, cache_keys, w_in = args[0], args[2], args[6], args[11]
+    seq_count, head_count = mesh.shape["seq"], mesh.shape["head"]
+    rows = tokens.shape[0] // (mesh.shape["rep"] * mesh.shape["sub"])
+    kv_local = cache_keys.shape[1] // head_count
+    group = w_query.shape[1] // (cache_keys.shape[1] * cache_keys.shape[3])
+    return (
+        rows == 8
+        and kv_local % 2 == 0
+        and group == 4
+        and kv_local * group * rows == 128
+        and cache_keys.shape[3] == 128
+        and tokens.shape[1] // seq_count % 512 == 0
+        and w_in.shape[2] // (seq_count * head_count) % 512 == 0
+    )
+
+
 def solution(mesh):
     in_specs = (
         P(("rep", "sub"), "seq"),
@@ -202,4 +778,13 @@
         P(("seq", "head"), None),
     )
     out_specs = (P(("rep", "sub"), "seq"), P(("rep", "sub"), None, ("seq", "head")))
-    return jax.shard_map(local, mesh=mesh, in_specs=in_specs, out_specs=out_specs, check_vma=False)
+
+    def run(*args):
+        body = local
+        if fits(mesh, args):
+            body = functools.partial(fused, mesh.shape["seq"], mesh.shape["head"])
+        return jax.shard_map(
+            body, mesh=mesh, in_specs=in_specs, out_specs=out_specs, check_vma=False
+        )(*args)
+
+    return run

time: 205 us -> 47.8 us (0.23)
  blocking collectives: 127 us -> 0 us
  Pallas kernels: 0 us -> 39.8 us
  waiting for transfers between devices: 31.3 us -> 0 us
  matrix products: 25.4 us -> 0 us
  between operations: 14.4 us -> 0.64 us
  local copies, waits for them, and re-layouts: 1.8 us -> 7.05 us
  other arithmetic: 4.82 us -> 0 us
    psum x4 -> x0, blocking collectives: 73.8 us -> none  [the longest x1 35.1 us: local(): projected = lax.psum(proj_part, ('seq', 'head'))]
    all_gather x4 -> x0, blocking collectives: 53.3 us -> none  [the longest x3 40.2 us: joined(): pieces = jax.tree.map(lambda part: lax.all_gather(part, axis), value)]
    pallas_call x0 -> x1, Pallas kernels: none -> 39.8 us  [fused(): pl.pallas_call(functools.partial(fused_kernel, seq_count, head_count), ou...]
    dot_general x11 -> x0, matrix products: 25.4 us -> none  [the longest x1 8.73 us: local(): mamba_part = jnp.dot(gated, w_mamba_out, preferred_element_type=jnp.float32)]
    reduce_scatter x1 -> x0, waiting for transfers between devices: 16.6 us -> none  [local(): lax.psum_scatter(mamba_part.astype(jnp.bfloat16), 'seq', scatter_dimensio...]
    psum x1 -> x0, waiting for transfers between devices: 14.7 us -> none  [local(): lax.psum((part_query, part_key, part_value), 'seq')]
    unnamed x34 -> x4, local copies, waits for them, and re-layouts: 0.09 us -> 7.05 us
  transfers between devices with their start and end apart: 2 -> 0, of which waited for: 2 -> 0; matrix products, arithmetic and copies ran while one was open for 1% -> 0% of each run, Pallas kernels for 0% -> 0%
where the time goes in v1:
time: 47.8 us; the launch traced here: 47.5 us
  Pallas kernels  39.8 us (83%)
  local copies, waits for them, and re-layouts  7.05 us (15%)
  between operations  0.64 us (1%)
    pallas_call x1, Pallas kernels, fused(): pl.pallas_call(functools.partial(fused_kernel, seq_count, head_count), ou...  39.8 us
    unnamed x4, local copies, waits for them, and re-layouts  7.05 us

profile of v1, /device:TPU:0, one launch (start us, length us, event | category | flops | bytes accessed | tf_op | source)
XLA Modules:
  0.0 47.5 jit_solution(4128865858946609124)
XLA Ops:
  0.6 1.6 %copy.24.cs_hbm = f32[8,3,1024]{2,1,0:T(4,128)} copy(f32[8,3,1024]{2,0,1:T(8,128)} %param.36) | data formatting | bytes 196608 | tf_op args[14]
  2.2 2.2 %copy.25.wx_hbm = bf16[1024,288]{1,0:T(8,128)(2,1)} copy(bf16[1024,288]{0,1:T(8,128)(2,1)} %param.37) | data formatting | bytes 1179648 | tf_op args[15]
  4.5 39.8 %shard_map.221 = (bf16[8,1024]{1,0:T(8,128)(2,1)}, f32[8,16,1024]{2,1,0:T(8,128)}) custom-call(s32[8]{0:T(128)} %length_ref.1, s32[8]{0:T(128)} %position_ref.1, bf16[8,1024]{1,0:T(8,128)(2,1)} %token_ref.1, f32[1024]{0:T(1024)} %attn_gain_ref.1, f32[4096]{0:T(1024)} %mamba_gain_ref.1, f32[4,1024]{1,0:T(4,128)} %conv_weight_ref.1, f32[1024]{0:T(1024)} %conv_bias_ref.1, ...), custom_call_target="tpu_custom_call" | custom-call | tf_op jit(solution)/shard_map/pallas_call | solution.py:723
  44.3 1.3 %copy.28 = bf16[8,1024]{1,0:T(8,128)(2,1)} copy(bf16[8,1024]{1,0:T(8,128)(2,1)} %get-tuple-element.4) | data formatting | bytes 32768
  45.6 1.9 %copy.29 = f32[8,16,1024]{2,1,0:T(8,128)} copy(f32[8,16,1024]{2,1,0:T(8,128)} %get-tuple-element.5) | data formatting | bytes 1048576

commit v2 on v1

--- a/solution.py
+++ b/solution.py
@@ -549,12 +549,14 @@
     taps = conv_weight_ref.shape[0]
     mixed = inner * conv_weight_ref[taps - 1 : taps, :] + conv_bias_ref[...][None, :]
     for k in range(taps - 1):
-        mixed = mixed + cs[:, k, :] * conv_weight_ref[k : k + 1, :]
+        mixed = mixed + cs[k] * conv_weight_ref[k : k + 1, :]
     u = mixed / (1.0 + jnp.exp(-mixed))
     ld_wx.wait()
-    proj_width = wx.shape[1]
-    proj_part[...] = jnp.zeros(proj_part.shape, f32)
-    proj_part[:, :proj_width] = dot(u.astype(bf16), wx[...])
+    proj_width = wx.shape[0]
+    proj_part[...] = jnp.zeros(proj_part.shape, bf16)
+    proj_part[:, :proj_width] = lax.dot_general(
+        u.astype(bf16), wx[...], (((1,), (1,)), ((), ())), preferred_element_type=f32
+    ).astype(bf16)
     order = list(enumerate(everyone))
 
     def all_copy(phase, index, ks, kh, src, slots):
@@ -578,9 +580,9 @@
     ld_state.wait()
     for index, (ks, kh) in order:
         all_copy(0, index, ks, kh, proj_part, proj_slots).wait_recv()
-    projected = proj_part[...]
+    projected = proj_part[...].astype(f32)
     for index, _ in order:
-        projected = projected + proj_slots[index]
+        projected = projected + proj_slots[index].astype(f32)
     low = dot(projected[:, :rank].astype(bf16), wdt[...]) + dt_bias_ref[...][None, :]
     dt = jnp.maximum(low, 0.0) + jnp.log1p(jnp.exp(-jnp.abs(low)))
     dtu = dt * u
@@ -663,6 +665,8 @@
     others = seq_count * head_count - 1
     f32 = jnp.float32
     bf16 = jnp.bfloat16
+    conv_state = jnp.transpose(conv_state, (1, 0, 2))
+    w_xproj = w_xproj.T
     big = (
         w_query,
         key_projection_weight,
@@ -704,8 +708,8 @@
         V((seq_count, rows, feature), bf16),
         V((seq_count, rows, feature), f32),
         V((2, rows, chan), f32),
-        V((rows, proj_pad), f32),
-        V((others, rows, proj_pad), f32),
+        V((rows, proj_pad), bf16),
+        V((others, rows, proj_pad), bf16),
         V((rows, chan), f32),
         V((rows, chan), bf16),
         V((seq_count, rows, feature), bf16),

time: 47.8 us -> 43.5 us (0.910)
  local copies, waits for them, and re-layouts: 7.05 us -> 3.21 us
    unnamed x4 -> x2, local copies, waits for them, and re-layouts: 7.05 us -> 3.21 us
where the time goes in v2:
time: 43.5 us; the launch traced here: 43.3 us
  Pallas kernels  39.4 us (91%)
  local copies, waits for them, and re-layouts  3.21 us (7%)
  between operations  0.65 us (1%)
    pallas_call x1, Pallas kernels, fused(): pl.pallas_call(functools.partial(fused_kernel, seq_count, head_count), ou...  39.4 us
    unnamed x2, local copies, waits for them, and re-layouts  3.21 us

profile of v2, /device:TPU:0, one launch (start us, length us, event | category | flops | bytes accessed | tf_op | source)
XLA Modules:
  0.0 43.3 jit_solution(13127766586622877908)
XLA Ops:
  0.6 39.4 %shard_map.221 = (bf16[8,1024]{1,0:T(8,128)(2,1)}, f32[8,16,1024]{2,1,0:T(8,128)}) custom-call(s32[8]{0:T(128)} %length_ref.1, s32[8]{0:T(128)} %position_ref.1, bf16[8,1024]{1,0:T(8,128)(2,1)} %token_ref.1, f32[1024]{0:T(1024)} %attn_gain_ref.1, f32[4096]{0:T(1024)} %mamba_gain_ref.1, f32[4,1024]{1,0:T(4,128)} %conv_weight_ref.1, f32[1024]{0:T(1024)} %conv_bias_ref.1, ...), custom_call_target="tpu_custom_call" | custom-call | tf_op jit(solution)/shard_map/pallas_call | solution.py:727
  40.1 1.3 %copy.26 = bf16[8,1024]{1,0:T(8,128)(2,1)} copy(bf16[8,1024]{1,0:T(8,128)(2,1)} %get-tuple-element.4) | data formatting | bytes 32768
  41.4 1.9 %copy.27 = f32[8,16,1024]{2,1,0:T(8,128)} copy(f32[8,16,1024]{2,1,0:T(8,128)} %get-tuple-element.5) | data formatting | bytes 1048576
